TPU v7x, 32 devices: a whole 2x2x4 slice. The times are simulated.
32 devices in a mesh: dp: 8 (over z, y), mp: 4 (over x, core).
Axes of the slice: x: 2, y: 2, z: 4, core: 2. Of those that a mesh axis runs over, the one named last changes fastest.
Arguments:
- tokens: bfloat16 [8, 1024, 1280], P('dp', 'mp'), may hold values from -6 to 6
- sizes: float32 [8, 1024], P('dp'), may hold values from 1 to 8
- ln1_gain: float32 [1280], replicated, may hold values from 0.25 to 1.75
- qkv_weight: bfloat16 [3, 1280, 1280], P(None, 'dp', 'mp'), may hold values from -0.15625 to 0.15625
- proj_weight: bfloat16 [1280, 1280], P('mp', 'dp'), may hold values from -0.15625 to 0.15625
- ln2_gain: float32 [1280], replicated, may hold values from 0.25 to 1.75
- fc1_weight: bfloat16 [1280, 5120], P('dp', 'mp'), may hold values from -0.15625 to 0.15625
- fc1_bias: float32 [5120], P('mp'), may hold values from -3 to 3
- fc2_weight: bfloat16 [5120, 1280], P('mp', 'dp'), may hold values from -0.078125 to 0.078125
- pair_source: int32 [8, 16], P('dp'), may hold values from 0 to 1022, as said below
- pair_target: int32 [8, 16], P('dp'), may hold values from 1 to 1023, as said below
- kept_order: int32 [8, 1008], P('dp'), may hold values from 0 to 1023, as said below
Outputs:
- merged_out: bfloat16 [8, 1008, 1280], P('dp', 'mp')
Inputs may be any that keep to these rules, and one draw needn't show every extreme that they name: `pair_source`: in each image the 16 entries are distinct even token indices. `pair_target`: odd token indices; several sources may join the same target. `kept_order`: in each image every token index that is not in pair_source appears exactly once.
All inputs are finite; a program needn't handle non-finite values.
Results may differ from a plain program's by a relative error of at most 0.017.
Values may be sent and summed in bfloat16 or wider, within the bound.
A program may use at most 64 MiB of HBM per device.

v0:
```python
import math
import jax
import jax.numpy as jnp
from jax import lax
from jax.sharding import PartitionSpec as P

D = 1280
HEADS = 16


def layer_norm(values, gain):
    center = values - jnp.mean(values, axis=-1, keepdims=True)
    spread = jnp.mean(center * center, axis=-1, keepdims=True)
    return center * lax.rsqrt(spread + 1e-06) * gain


def merge_rows(total, order_rows, source_ids, target_ids):
    kept_rows = jnp.take_along_axis(total, order_rows[:, :, None], axis=1)
    source_rows = jnp.take_along_axis(total, source_ids[:, :, None], axis=1)
    joins = (order_rows[:, :, None] == target_ids[:, None, :]).astype(jnp.float32)
    return kept_rows + jnp.einsum(
        "icr,ird->icd", joins, source_rows, precision=lax.Precision.HIGHEST
    )


def shards(
    tokens,
    sizes,
    ln1_gain,
    qkv_weight,
    proj_weight,
    ln2_gain,
    fc1_weight,
    fc1_bias,
    fc2_weight,
    pair_source,
    pair_target,
    kept_order,
):
    images, own_tokens, width = tokens.shape
    length = sizes.shape[1]
    kept_total = kept_order.shape[1]
    devices_mp = lax.axis_size("mp")
    own_start = lax.axis_index("mp") * own_tokens
    head_size = D // HEADS
    base = tokens.astype(jnp.float32)
    normed = layer_norm(base, ln1_gain).astype(jnp.bfloat16)
    whole = lax.all_gather(normed, "mp", axis=1, tiled=True)
    local_width = qkv_weight.shape[2]
    columns = whole
    projected = jnp.einsum(
        "ind,cdf->cinf",
        columns,
        lax.all_gather(qkv_weight, "dp", axis=1, tiled=True),
        preferred_element_type=jnp.float32,
    ).astype(jnp.bfloat16)
    local_heads = local_width // head_size
    shaped = projected.reshape(3, images, length, local_heads, head_size)
    queries = shaped[0]
    keys_all = shaped[1]
    values_all = shaped[2]
    size_bias = jnp.log(sizes)[:, None, None, :]
    block = min(512, length)
    outputs = []
    for begin in range(0, length, block):
        scores = (
            jnp.einsum(
                "iqhe,ikhe->ihqk",
                queries[:, begin : begin + block],
                keys_all,
                preferred_element_type=jnp.float32,
            )
            / math.sqrt(head_size)
            + size_bias
        )
        weights = jax.nn.softmax(scores, axis=-1).astype(jnp.bfloat16)
        attended_block = jnp.einsum(
            "ihqk,ikhe->iqhe", weights, values_all, preferred_element_type=jnp.float32
        )
        outputs.append(attended_block.astype(jnp.bfloat16).reshape(images, block, local_width))
    attended = jnp.concatenate(outputs, axis=1)
    branch = jnp.einsum(
        "ind,de->ine",
        attended,
        lax.all_gather(proj_weight, "dp", axis=1, tiled=True),
        preferred_element_type=jnp.float32,
    )
    weighted = sizes[:, :, None] * branch
    own_sizes = lax.dynamic_slice_in_dim(sizes, own_start, own_tokens, 1)
    own_weighted = own_sizes[:, :, None] * base
    local_total = lax.dynamic_update_slice_in_dim(
        weighted,
        lax.dynamic_slice_in_dim(weighted, own_start, own_tokens, 1) + own_weighted,
        own_start,
        1,
    )
    merged_count = kept_total // devices_mp
    own_order = lax.dynamic_slice_in_dim(
        kept_order, lax.axis_index("mp") * merged_count, merged_count, 1
    )
    scattered = lax.psum_scatter(
        jnp.transpose(
            merge_rows(local_total, kept_order, pair_source, pair_target), (1, 0, 2)
        ).astype(jnp.bfloat16),
        "mp",
        scatter_dimension=0,
        tiled=True,
    ).astype(jnp.float32)
    numerator = jnp.transpose(scattered, (1, 0, 2))
    merged_size = merge_rows(sizes[:, :, None], own_order, pair_source, pair_target)
    merged = numerator / merged_size
    normed_two = layer_norm(merged, ln2_gain).astype(jnp.bfloat16)
    gathered = lax.all_gather(normed_two, "mp", axis=1, tiled=True)
    columns = gathered
    hidden_sum = jnp.einsum(
        "imd,df->imf",
        columns,
        lax.all_gather(fc1_weight, "dp", axis=0, tiled=True),
        preferred_element_type=jnp.float32,
    )
    hidden = jax.nn.gelu(hidden_sum + fc1_bias).astype(jnp.bfloat16)
    partial_out = jnp.einsum(
        "imf,fd->imd",
        hidden,
        lax.all_gather(fc2_weight, "dp", axis=1, tiled=True),
        preferred_element_type=jnp.float32,
    )
    mlp_part = lax.psum_scatter(
        partial_out.astype(jnp.bfloat16), "mp", scatter_dimension=1, tiled=True
    ).astype(jnp.float32)
    return (merged + mlp_part).astype(jnp.bfloat16)


def solution(mesh):
    return jax.shard_map(
        shards,
        mesh=mesh,
        in_specs=(
            P("dp", "mp", None),
            P("dp", None),
            P(),
            P(None, "dp", "mp"),
            P("mp", "dp"),
            P(),
            P("dp", "mp"),
            P("mp"),
            P("mp", "dp"),
            P("dp", None),
            P("dp", None),
            P("dp", None),
        ),
        out_specs=P("dp", "mp", None),
        check_vma=False,
    )
```

profile of v0, /device:TPU:1, one launch (start us, length us, event | category | flops | bytes accessed | tf_op | source)
XLA Modules:
  0.0 317.7 jit_solution(4380768634615341311)
XLA Ops:
  6.5 0.0 all-gather.6.cloned.1.call-start
  6.6 1.3 convert_reduce_fusion
  7.9 0.0 copy-start.5
  7.9 1.4 fusion.30
  9.3 2.2 fusion.32
  11.5 0.0 all-gather.6.cloned.1.call-update
  11.6 0.0 all-gather.8.cloned.1.call-start
  11.6 0.7 all-gather.8.cloned.1.call-update
  12.3 0.0 all-gather.12.cloned.1.call-start
  12.4 0.7 all-gather.12.cloned.1.call-update
  13.0 0.0 all-gather.14.cloned.1.call-start
  13.1 0.5 all-gather.14.cloned.1.call-update
  13.6 0.0 all-gather.10.cloned.1.call-start
  13.7 0.0 copy-done.8
  13.7 0.0 copy-done
  13.7 0.0 copy-done.2
  13.8 28.3 %all_gather.20 = bf16[320,1280]{0,1:T(8,128)(2,1)S(1)} all-gather(bf16[320,160]{0,1:T(8,128)(2,1)S(1)} %copy-done.2), channel_id=1, replica_groups=mesh['dp'=8,'mp'=4] {'dp'}, dimensions={1}, use_global_device_ids=true | all-gather | bytes 921600 | tf_op jit(solution)/shard_map/all_gather | solution.py:85
  42.0 0.0 copy-done.3
  42.1 0.1 compare_select_fusion.2
  42.2 0.6 gather_fusion.3
  42.8 1.4 gather_fusion.2
  44.2 0.0 copy-done.5
  44.2 0.2 fusion.56
  44.4 53.4 %all-gather.8.cloned.1.call-done = bf16[3,1280,320]{2,1,0:T(8,128)(2,1)} async-done(((bf16[3,160,320]{2,1,0:T(8,128)(2,1)}), bf16[3,1280,320]{2,1,0:T(8,128)(2,1)}) %all-gather.8.cloned.1.call-update) | async-done | bytes 2457616 | tf_op jit(solution)/shard_map/all_gather | solution.py:54
  97.8 5.4 %convert_bitcast_fusion = bf16[3,1,1024,320]{2,3,0,1:T(8,128)(2,1)S(1)} fusion(bf16[3,1280,320]{2,1,0:T(8,128)(2,1)} %all-gather.8.cloned.1.call-done, bf16[1,1024,1280]{2,1,0:T(8,128)(2,1)} %all-gather.6.cloned.1.call-done), kind=kOutput, calls=%fused_computation.38 | convolution fusion | flops 2517565440 | bytes 7045120 | tf_op jit(solution)/shard_map/ind,cdf->cinf/dot_general | solution.py:51
  103.2 0.2 fusion.78
  103.3 4.9 %fusion.80 = (f32[4,512]{1,0:T(4,128)S(1)}, f32[4,512,1024]{2,1,0:T(8,128)}) fusion(f32[1024]{0:T(1024)S(1)} %bitcast.179, bf16[1024,4,80]{0,2,1:T(8,128)(2,1)S(1)} %bitcast.170, bf16[1,1024,4,80]{1,3,2,0:T(8,128)(2,1)S(1)} %bitcast.168), kind=kOutput, calls=%fused_computation.120 | convolution fusion | flops 343933952 | bytes 9383936 | tf_op jit(solution)/shard_map/sub | solution.py:76
  108.2 4.9 %fusion.79 = (f32[4,512]{1,0:T(4,128)S(1)}, f32[4,512,1024]{2,1,0:T(8,128)}) fusion(f32[1024]{0:T(1024)S(1)} %bitcast.180, bf16[1024,4,80]{0,2,1:T(8,128)(2,1)S(1)} %bitcast.171, bf16[1,1024,4,80]{1,3,2,0:T(8,128)(2,1)S(1)} %bitcast.169), kind=kOutput, calls=%fused_computation.119 | convolution fusion | flops 343933952 | bytes 9383936 | tf_op jit(solution)/shard_map/sub | solution.py:76
  113.0 5.1 %fusion.37 = bf16[4,80,512]{2,1,0:T(8,128)(2,1)S(1)} fusion(bf16[1024,4,80]{0,2,1:T(8,128)(2,1)S(1)} %bitcast.166, f32[4,512,1024]{2,1,0:T(8,128)} %get-tuple-element.13, f32[4,512]{1,0:T(4,128)S(1)} %get-tuple-element.12), kind=kOutput, calls=%fused_computation.55 | convolution fusion | flops 339902464 | bytes 9379840 | tf_op jit(solution)/shard_map/ihqk,ikhe->iqhe/dot_general | solution.py:77
  118.1 0.8 copy-done.9
  118.9 1.7 fusion.36
  120.6 0.0 copy-start.1
  120.6 4.0 %convolution_multiply_fusion = f32[1024,1280]{1,0:T(8,128)} fusion(bf16[320,1280]{0,1:T(8,128)(2,1)S(1)} %all_gather.20, f32[1024]{0:T(1024)S(1)} %bitcast.165, bf16[1,512,320]{1,2,0:T(8,128)(2,1)S(1)} %bitcast.173, bf16[1,512,320]{1,2,0:T(8,128)(2,1)S(1)} %bitcast.172), kind=kOutput, calls=%fused_computation.24 | convolution fusion | flops 841482240 | bytes 6721536 | tf_op jit(solution)/shard_map/ind,de->ine/dot_general | solution.py:82
  124.6 1.4 constant_dynamic-slice_fusion.2
  126.0 0.0 copy-done.1
  126.0 1.3 fusion.35
  127.3 3.1 gather_fusion.1
  130.5 9.7 %gather_fusion = f32[1008,1280]{1,0:T(8,128)} fusion(f32[1024,1280]{1,0:T(8,128)} %fusion.35, s32[1024]{0:T(1024)S(1)} %pad_clamp_fusion.2), kind=kCustom, calls=%fused_computation | custom fusion | bytes 10325952 | tf_op jit(solution)/shard_map/jit(take_along_axis)/gather | solution.py:18
  140.1 5.1 %fusion.21 = bf16[1008,1,1280]{2,0,1:T(8,128)(2,1)S(1)} fusion(f32[1008,1280]{1,0:T(8,128)} %gather_fusion, pred[1008]{0:T(1024)(128)(4,1)S(1)} %compare_and_fusion, f32[16,1280]{1,0:T(8,128)S(1)} %gather_fusion.1, pred[16]{0:T(512)(128)(4,1)S(1)} %compare_and_fusion.1, s32[1008]{0:T(1024)S(1)} %bitcast.175, s32[16]{0:T(128)S(1)} %bitcast.185), kind=kOutput, calls=%fused_computation.33 | convolution fusion | flops 251633408 | bytes 7828480 | tf_op jit(solution)/shard_map/icr,ird->icd/dot_general | solution.py:21
  145.2 0.0 copy-start.6
  145.2 0.0 copy-start.4
  145.2 27.6 %fusion = bf16[256,1280]{1,0:T(8,128)(2,1)S(1)} fusion(bf16[1008,1,1280]{2,0,1:T(8,128)(2,1)S(1)} %fusion.21), kind=kCustom, calls=%all-reduce-scatter | all-reduce-scatter fusion | flops 1310721 | bytes 3236352
  172.8 4.4 %collective-permute-start = (bf16[12,1280]{1,0:T(8,128)(2,1)S(1)}, bf16[12,1280]{1,0:T(8,128)(2,1)S(1)}, u32[]{:S(2)}, u32[]{:S(2)}) collective-permute-start(bf16[12,1280]{1,0:T(8,128)(2,1)S(1)} %slice.36), channel_id=1, source_target_pairs={{0,1},{1,2},{2,3},{4,5},{5,6},{6,7},{8,9},{9,10},{10,11},{12,13},{... | collective-permute-start | bytes 92168
  177.2 0.0 copy-done.6
  177.2 0.6 dynamic-slice.10
  178.5 0.0 collective-permute-done
  178.5 1.1 concatenate.4
  179.6 0.0 copy-start.7
  179.6 0.4 fusion.46
  180.0 0.5 multiply_reduce_fusion
  180.5 0.0 copy-done.4
  180.5 0.4 multiply_convert_fusion
  180.9 2.1 copy.14
  183.0 0.0 all-gather.10.cloned.1.call-update
  183.0 0.0 all-gather.12.cloned.1.call-done
  183.1 39.2 %all-gather.14.cloned.1.call-done = bf16[1280,1280]{0,1:T(8,128)(2,1)} async-done(((bf16[1280,160]{0,1:T(8,128)(2,1)}), bf16[1280,1280]{0,1:T(8,128)(2,1)}) %all-gather.14.cloned.1.call-update) | async-done | bytes 3276816 | tf_op jit(solution)/shard_map/all_gather | solution.py:125
  222.2 42.2 %all-gather.10.cloned.1.call-done = bf16[1,1008,1280]{2,0,1:T(2,128)(2,1)} async-done(((bf16[1,252,1280]{2,0,1:T(2,128)(2,1)}), bf16[1,1008,1280]{2,0,1:T(2,128)(2,1)}) %all-gather.10.cloned.1.call-update) | async-done | bytes 2580496 | tf_op jit(solution)/shard_map/all_gather | solution.py:113
  264.5 0.0 copy-done.7
  264.5 12.8 %fusion.20 = bf16[1,1008,1280]{2,1,0:T(8,128)(2,1)} fusion(bf16[1280,1280]{0,1:T(8,128)(2,1)} %all-gather.14.cloned.1.call-done, bf16[1280,1280]{1,0:T(8,128)(2,1)} %all-gather.12.cloned.1.call-done, bf16[1,1008,1280]{2,0,1:T(2,128)(2,1)} %all-gather.10.cloned.1.call-done, f32[1280]{0:T(1024)S(1)} %copy-done.7), kind=kOutput, calls=%fused_computation.32 | convolution fusion | flops 6620221440 | bytes 11719680 | tf_op jit(solution)/shard_map/imf,fd->imd/dot_general | solution.py:122
  277.3 26.0 %fusion.1 = bf16[256,1280]{1,0:T(8,128)(2,1)S(1)} fusion(bf16[1,1008,1280]{2,1,0:T(8,128)(2,1)} %fusion.20), kind=kCustom, calls=%all-reduce-scatter.1 | all-reduce-scatter fusion | flops 1310721 | bytes 3236352
  303.4 4.4 %collective-permute-start.1 = (bf16[12,1280]{1,0:T(8,128)(2,1)S(1)}, bf16[12,1280]{1,0:T(8,128)(2,1)S(1)}, u32[]{:S(2)}, u32[]{:S(2)}) collective-permute-start(bf16[12,1280]{1,0:T(8,128)(2,1)S(1)} %slice.37), channel_id=1, source_target_pairs={{0,1},{1,2},{2,3},{4,5},{5,6},{6,7},{8,9},{9,10},{10,11},{12,13},{... | collective-permute-start | bytes 92168
  307.8 1.1 collective-permute-done.1
  308.9 1.0 concatenate.5
  309.9 1.3 add_convert_fusion.1
  (22 shorter events, 0.1 us)
Async XLA Ops:
  6.5 7.1 %copy-start.8 = (s32[1,16]{1,0:T(1,128)S(1)}, s32[1,16]{1,0:T(1,128)}, u32[]{:S(2)}) copy-start(s32[1,16]{1,0:T(1,128)} %param.21) | copy-start | bytes 196
  6.5 7.2 %copy-start = (f32[1,1024]{1,0:T(1,128)S(1)}, f32[1,1024]{1,0:T(1,128)}, u32[]{:S(2)}) copy-start(f32[1,1024]{1,0:T(1,128)} %param.13) | copy-start | bytes 12292
  6.5 7.2 %copy-start.2 = (bf16[320,160]{0,1:T(8,128)(2,1)S(1)}, bf16[320,160]{0,1:T(8,128)(2,1)}, u32[]{:S(2)}) copy-start(bf16[320,160]{0,1:T(8,128)(2,1)} %param.16) | copy-start | bytes 307204
  6.5 35.5 %copy-start.3 = (s32[1,1008]{1,0:T(1,128)S(1)}, s32[1,1008]{1,0:T(1,128)}, u32[]{:S(2)}) copy-start(s32[1,1008]{1,0:T(1,128)} %param.23) | copy-start | bytes 12100
  6.5 37.8 %all-gather.6.cloned.1.call-start = ((), (), s32[]{:S(2)}) async-start(), calls=%async_computation | async-start | bytes 3276800 | tf_op jit(solution)/shard_map/all_gather | solution.py:48
  7.9 36.3 %copy-start.5 = (s32[1,16]{1,0:T(1,128)S(1)}, s32[1,16]{1,0:T(1,128)}, u32[]{:S(2)}) copy-start(s32[1,16]{1,0:T(1,128)} %param.22) | copy-start | bytes 196
  11.6 86.2 %all-gather.8.cloned.1.call-start = ((), (), s32[]{:S(2)}) async-start(), calls=%async_computation.1 | async-start | bytes 3317760 | tf_op jit(solution)/shard_map/all_gather | solution.py:54
  12.3 170.7 %all-gather.12.cloned.1.call-start = ((), (), s32[]{:S(2)}) async-start(), calls=%async_computation.3 | async-start | bytes 3686400 | tf_op jit(solution)/shard_map/all_gather | solution.py:118
  13.0 209.2 %all-gather.14.cloned.1.call-start = ((), (), s32[]{:S(2)}) async-start(), calls=%async_computation.4 | async-start | bytes 3686400 | tf_op jit(solution)/shard_map/all_gather | solution.py:125
  13.6 250.8 %all-gather.10.cloned.1.call-start = ((), (), s32[]{:S(2)}) async-start(), calls=%async_computation.2 | async-start | bytes 6451200 | tf_op jit(solution)/shard_map/all_gather | solution.py:113
  113.0 5.9 %copy-start.9 = (f32[4,512,1024]{2,1,0:T(8,128)S(1)}, f32[4,512,1024]{2,1,0:T(8,128)}, u32[]{:S(2)}) copy-start(f32[4,512,1024]{2,1,0:T(8,128)} %get-tuple-element.11) | copy-start | bytes 25165828
  120.6 5.4 %copy-start.1 = (bf16[1,256,1280]{2,1,0:T(8,128)(2,1)S(1)}, bf16[1,256,1280]{2,1,0:T(8,128)(2,1)}, u32[]{:S(2)}) copy-start(bf16[1,256,1280]{2,1,0:T(8,128)(2,1)} %param.12) | copy-start | bytes 1966084
  145.2 32.0 %copy-start.6 = (u32[32]{0:T(128)S(1)}, u32[32]{0:T(128)}, u32[]{:S(2)}) copy-start(u32[32]{0:T(128)} %constant.99) | copy-start | bytes 388
  145.2 35.3 %copy-start.4 = (f32[1280]{0:T(1024)S(1)}, f32[1280]{0:T(1024)}, u32[]{:S(2)}) copy-start(f32[1280]{0:T(1024)} %param.17) | copy-start | bytes 15364
  172.8 5.7 %collective-permute-start = (bf16[12,1280]{1,0:T(8,128)(2,1)S(1)}, bf16[12,1280]{1,0:T(8,128)(2,1)S(1)}, u32[]{:S(2)}, u32[]{:S(2)}) collective-permute-start(bf16[12,1280]{1,0:T(8,128)(2,1)S(1)} %slice.36), channel_id=1, source_target_pairs={{0,1},{1,2},{2,3},{4,5},{5,6},{6,7},{8,9},{9,10},{10,11},{12,13},{... | collective-permute-start | bytes 92168
  179.6 84.9 %copy-start.7 = (f32[1280]{0:T(1024)S(1)}, f32[1280]{0:T(1024)}, u32[]{:S(2)}) copy-start(f32[1280]{0:T(1024)} %param.19) | copy-start | bytes 15364
  303.4 5.5 %collective-permute-start.1 = (bf16[12,1280]{1,0:T(8,128)(2,1)S(1)}, bf16[12,1280]{1,0:T(8,128)(2,1)S(1)}, u32[]{:S(2)}, u32[]{:S(2)}) collective-permute-start(bf16[12,1280]{1,0:T(8,128)(2,1)S(1)} %slice.37), channel_id=1, source_target_pairs={{0,1},{1,2},{2,3},{4,5},{5,6},{6,7},{8,9},{9,10},{10,11},{12,13},{... | collective-permute-start | bytes 92168
Sparse Core Ops, SparseCore 0:
  11.7 27.9 all-gather.5
  41.9 55.8 all-gather.7
  100.0 59.9 all-gather.11
  162.0 60.1 all-gather.13
  223.6 40.7 all-gather.9
where the time goes:
time: 318 us
  waiting for transfers between devices  138 us (43%)
  blocking collectives  81.9 us (26%)
  matrix products  44 us (14%)
  local copies, waits for them, and re-layouts  22 us (7%)
  between operations  14.1 us (4%)
  starting transfers between devices  8.96 us (3%)
  other arithmetic  8.93 us (3%)
    unnamed x2, blocking collectives  53.6 us
    all_gather x1, waiting for transfers between devices, shards(): lax.all_gather(qkv_weight, 'dp', axis=1, tiled=True)  53.4 us
    all_gather x1, waiting for transfers between devices, shards(): gathered = lax.all_gather(normed_two, 'mp', axis=1, tiled=True)  42.2 us
    all_gather x1, waiting for transfers between devices, shards(): lax.all_gather(fc2_weight, 'dp', axis=1, tiled=True)  39.2 us
    all_gather x1, blocking collectives, shards(): lax.all_gather(proj_weight, 'dp', axis=1, tiled=True)  28.3 us
    dot_general x1, matrix products, shards(): jnp.einsum('imf,fd->imd', hidden, lax.all_gather(fc2_weight, 'dp', axis=1...  12.8 us
    gather x2, local copies, waits for them, and re-layouts, merge_rows(): kept_rows = jnp.take_along_axis(total, order_rows[:, :, None], axis=1)  11 us
    sub x2, matrix products, shards(): weights = jax.nn.softmax(scores, axis=-1).astype(jnp.bfloat16)  9.7 us
  transfers between devices with their start and end apart: 7, of which 4 were waited for; matrix products, arithmetic and copies ran while one was open for 26% of the time, Pallas kernels for 0%

commit v1 on v0

--- a/solution.py
+++ b/solution.py
@@ -3,6 +3,7 @@
 import jax.numpy as jnp
 from jax import lax
 from jax.sharding import PartitionSpec as P
+from jax.lax import axis_index, axis_size, ppermute
 
 D = 1280
 HEADS = 16
@@ -37,6 +38,41 @@
     pair_target,
     kept_order,
 ):
+
+    def reach_sizes(here_x, comm_axis, xin):
+        clean = axis_size(comm_axis)
+        latest, aux, raw_out = (clean, axis_index(comm_axis), here_x.shape[1])
+        k_now = map(lambda pp: (pp, (pp + 1) % latest), range(latest))
+        bank = list(k_now)
+        sides = [(i, w) for w, i in bank]
+        arr_out = ppermute(here_x, comm_axis, bank)
+        v_now = ppermute(here_x, comm_axis, sides)
+        finding, z1 = (arr_out, v_now)
+        v1 = xin(here_x, aux * raw_out)
+        reached = v1.shape[2]
+        block_last = jnp.zeros((*v1.shape[:2], latest * reached, *v1.shape[3:]), v1.dtype)
+
+        def process_wall_for(block_last, v1, field_out):
+            fresh = lax.dynamic_update_slice_in_dim(block_last, v1, field_out * reached, axis=2)
+            return fresh
+
+        block_last = process_wall_for(block_last, v1, aux)
+        kk = 1
+        while kk < latest // 2 + 1:
+            passed, all_rows = ((aux - kk) % latest, (aux + kk) % latest)
+            local_now = (finding, z1)
+            if kk < latest // 2:
+                y2 = ppermute(finding, comm_axis, bank)
+                view_out = ppermute(z1, comm_axis, sides)
+                finding, z1 = (y2, view_out)
+            high = xin(local_now[0], passed * raw_out)
+            block_last = process_wall_for(block_last, high, passed)
+            if 2 * kk < latest:
+                oldest = xin(local_now[1], all_rows * raw_out)
+                block_last = process_wall_for(block_last, oldest, all_rows)
+            kk += 1
+        return block_last
+
     images, own_tokens, width = tokens.shape
     length = sizes.shape[1]
     kept_total = kept_order.shape[1]
@@ -79,11 +115,12 @@
         )
         outputs.append(attended_block.astype(jnp.bfloat16).reshape(images, block, local_width))
     attended = jnp.concatenate(outputs, axis=1)
-    branch = jnp.einsum(
-        "ind,de->ine",
-        attended,
-        lax.all_gather(proj_weight, "dp", axis=1, tiled=True),
-        preferred_element_type=jnp.float32,
+    branch = reach_sizes(
+        proj_weight,
+        "dp",
+        lambda own_block, start: jnp.einsum(
+            "ind,de->ine", attended, own_block, preferred_element_type=jnp.float32
+        ),
     )
     weighted = sizes[:, :, None] * branch
     own_sizes = lax.dynamic_slice_in_dim(sizes, own_start, own_tokens, 1)

time: 318 us -> 335 us (1.053)
  local copies, waits for them, and re-layouts: 22 us -> 74.2 us
  blocking collectives: 81.9 us -> 53.3 us
  waiting for transfers between devices: 138 us -> 110 us
  starting transfers between devices: 8.96 us -> 22.6 us
  other arithmetic: 8.93 us -> 14.6 us
    dynamic_update_slice x0 -> x8, local copies, waits for them, and re-layouts: none -> 50 us  [process_wall_for(): lax.dynamic_update_slice_in_dim(block_last, v1, field_out * reached, axis=2)]
    all_gather x1, waiting for transfers between devices: 39.2 us -> 0.02 us  [shards(): lax.all_gather(fc2_weight, 'dp', axis=1, tiled=True)]
    all_gather x1 -> x0, blocking collectives: 28.3 us -> none  [shards(): lax.all_gather(proj_weight, 'dp', axis=1, tiled=True)]
    ppermute x0 -> x7, starting transfers between devices: none -> 13.6 us  [the longest x2 8.42 us: reach_sizes(): view_out = ppermute(z1, comm_axis, sides)]
    all_gather x1, waiting for transfers between devices: 0.01 us -> 5.45 us  [shards(): whole = lax.all_gather(normed, 'mp', axis=1, tiled=True)]
    ppermute x0 -> x7, waiting for transfers between devices: none -> 4.81 us  [the longest x3 4.52 us: reach_sizes(): y2 = ppermute(finding, comm_axis, bank)]
    all_gather x1, waiting for transfers between devices: 53.4 us -> 58.1 us  [shards(): lax.all_gather(qkv_weight, 'dp', axis=1, tiled=True)]
  transfers between devices with their start and end apart: 7 -> 14, of which waited for: 4 -> 7; matrix products, arithmetic and copies ran while one was open for 26% -> 41% of each run, Pallas kernels for 0% -> 0%
where the time goes in v1:
time: 335 us; the launch traced here: 333 us
  waiting for transfers between devices  110 us (33%)
  local copies, waits for them, and re-layouts  74.2 us (22%)
  blocking collectives  53.3 us (16%)
  matrix products  43.9 us (13%)
  starting transfers between devices  22.6 us (7%)
  other arithmetic  14.6 us (4%)
  between operations  14.4 us (4%)
    all_gather x1, waiting for transfers between devices, shards(): lax.all_gather(qkv_weight, 'dp', axis=1, tiled=True)  58.1 us
    unnamed x2, blocking collectives  53.3 us
    dynamic_update_slice x8, local copies, waits for them, and re-layouts, process_wall_for(): lax.dynamic_update_slice_in_dim(block_last, v1, field_out * reached, axis=2)  50 us
    all_gather x1, waiting for transfers between devices, shards(): gathered = lax.all_gather(normed_two, 'mp', axis=1, tiled=True)  39.4 us
    dot_general x1, matrix products, shards(): jnp.einsum('imf,fd->imd', hidden, lax.all_gather(fc2_weight, 'dp', axis=1...  12.9 us
    gather x2, local copies, waits for them, and re-layouts, merge_rows(): kept_rows = jnp.take_along_axis(total, order_rows[:, :, None], axis=1)  10.9 us
    sub x2, matrix products, shards(): weights = jax.nn.softmax(scores, axis=-1).astype(jnp.bfloat16)  9.88 us
    unnamed x2, starting transfers between devices  8.77 us
  transfers between devices with their start and end apart: 14, of which 7 were waited for; matrix products, arithmetic and copies ran while one was open for 41% of the time, Pallas kernels for 0%

profile of v1, /device:TPU:1, one launch (start us, length us, event | category | flops | bytes accessed | tf_op | source)
XLA Modules:
  0.0 333.3 jit_solution(13418143411827825330)
XLA Ops:
  6.6 1.3 convert_reduce_fusion
  7.9 1.4 fusion.30
  9.3 2.2 fusion.32
  11.6 0.7 all-gather.8.cloned.1.call-update
  12.4 0.7 all-gather.12.cloned.1.call-update
  13.1 2.1 collective-permute-start
  15.2 3.1 collective-permute-start.1
  18.6 0.1 compare_select_fusion.2
  18.7 0.6 gather_fusion.3
  19.4 0.2 fusion.54
  19.6 1.4 gather_fusion.2
  21.0 0.3 collective-permute-done
  21.3 4.2 %collective-permute-start.3 = (bf16[320,160]{0,1:T(8,128)(2,1)S(1)}, bf16[320,160]{0,1:T(8,128)(2,1)S(1)}, u32[]{:S(2)}, u32[]{:S(2)}) collective-permute-start(bf16[320,160]{0,1:T(8,128)(2,1)S(1)} %collective-permute-done.1), channel_id=1, source_target_pairs={{4,0},{8,4},{12,8},{16,12},{20,16},{24,20},{28,24},{0,28},{5,1},{9... | collective-permute-start | bytes 307208 | tf_op jit(solution)/shard_map/ppermute | solution.py:66
  25.5 2.3 collective-permute-done.2
  27.8 4.2 %collective-permute-start.5 = (bf16[320,160]{0,1:T(8,128)(2,1)S(1)}, bf16[320,160]{0,1:T(8,128)(2,1)S(1)}, u32[]{:S(2)}, u32[]{:S(2)}) collective-permute-start(bf16[320,160]{0,1:T(8,128)(2,1)S(1)} %collective-permute-done.3), channel_id=1, source_target_pairs={{4,0},{8,4},{12,8},{16,12},{20,16},{24,20},{28,24},{0,28},{5,1},{9... | collective-permute-start | bytes 307208 | tf_op jit(solution)/shard_map/ppermute | solution.py:66
  32.0 2.2 collective-permute-done.4
  34.3 5.5 %all-gather.6.cloned.1.call-done = bf16[1,1024,1280]{2,1,0:T(8,128)(2,1)} async-done(((bf16[1,256,1280]{2,1,0:T(8,128)(2,1)}), bf16[1,1024,1280]{2,1,0:T(8,128)(2,1)}) %all-gather.6.cloned.1.call-update) | async-done | bytes 2621456 | tf_op jit(solution)/shard_map/all_gather | solution.py:84
  39.7 58.1 %all-gather.8.cloned.1.call-done = bf16[3,1280,320]{2,1,0:T(8,128)(2,1)} async-done(((bf16[3,160,320]{2,1,0:T(8,128)(2,1)}), bf16[3,1280,320]{2,1,0:T(8,128)(2,1)}) %all-gather.8.cloned.1.call-update) | async-done | bytes 2457616 | tf_op jit(solution)/shard_map/all_gather | solution.py:90
  97.8 5.4 %convert_bitcast_fusion = bf16[3,1,1024,320]{2,3,0,1:T(8,128)(2,1)S(1)} fusion(bf16[3,1280,320]{2,1,0:T(8,128)(2,1)} %all-gather.8.cloned.1.call-done, bf16[1,1024,1280]{2,1,0:T(8,128)(2,1)} %all-gather.6.cloned.1.call-done), kind=kOutput, calls=%fused_computation.38 | convolution fusion | flops 2517565440 | bytes 7045120 | tf_op jit(solution)/shard_map/ind,cdf->cinf/dot_general | solution.py:87
  103.2 0.2 fusion.75
  103.3 5.0 %fusion.77 = (f32[4,512]{1,0:T(4,128)S(1)}, f32[4,512,1024]{2,1,0:T(8,128)}) fusion(f32[1024]{0:T(1024)S(1)} %bitcast.224, bf16[1024,4,80]{0,2,1:T(8,128)(2,1)S(1)} %bitcast.217, bf16[1,1024,4,80]{1,3,2,0:T(8,128)(2,1)S(1)} %bitcast.215), kind=kOutput, calls=%fused_computation.124 | convolution fusion | flops 343933952 | bytes 9383936 | tf_op jit(solution)/shard_map/sub | solution.py:112
  108.3 4.9 %fusion.76 = (f32[4,512]{1,0:T(4,128)S(1)}, f32[4,512,1024]{2,1,0:T(8,128)}) fusion(f32[1024]{0:T(1024)S(1)} %bitcast.225, bf16[1024,4,80]{0,2,1:T(8,128)(2,1)S(1)} %bitcast.218, bf16[1,1024,4,80]{1,3,2,0:T(8,128)(2,1)S(1)} %bitcast.216), kind=kOutput, calls=%fused_computation.123 | convolution fusion | flops 343933952 | bytes 9383936 | tf_op jit(solution)/shard_map/sub | solution.py:112
  113.2 5.1 %fusion.37 = bf16[4,80,512]{2,1,0:T(8,128)(2,1)S(1)} fusion(bf16[1024,4,80]{0,2,1:T(8,128)(2,1)S(1)} %bitcast.213, f32[4,512,1024]{2,1,0:T(8,128)} %get-tuple-element.13, f32[4,512]{1,0:T(4,128)S(1)} %get-tuple-element.12), kind=kOutput, calls=%fused_computation.63 | convolution fusion | flops 339902464 | bytes 9379840 | tf_op jit(solution)/shard_map/ihqk,ikhe->iqhe/dot_general | solution.py:113
  118.3 0.8 copy-done.10
  119.1 1.7 fusion.36
  120.8 0.5 convolution_bitcast_fusion.7
  121.3 2.6 broadcast_in_dim.68
  123.9 5.9 %dynamic_update_slice.27 = f32[1,1024,1280]{2,1,0:T(8,128)} dynamic-update-slice(f32[1,1024,1280]{2,1,0:T(8,128)} %broadcast_in_dim.68, f32[1,1024,160]{2,1,0:T(8,128)S(1)} %convolution_bitcast_fusion.7, s32[]{:T(128)} %constant.122.clone.1, s32[]{:T(128)} %constant.122.clone.1, s32[]{:T(128)S(6)} %select_n.205) | dynamic-update-slice | bytes 1310724 | tf_op jit(solution)/shard_map/dynamic_update_slice | solution.py:56
  129.8 0.5 convolution_bitcast_fusion.6
  130.2 5.9 %dynamic_update_slice.28 = f32[1,1024,1280]{2,1,0:T(8,128)} dynamic-update-slice(f32[1,1024,1280]{2,1,0:T(8,128)} %dynamic_update_slice.27, f32[1,1024,160]{2,1,0:T(8,128)S(1)} %convolution_bitcast_fusion.6, s32[]{:T(128)} %constant.122.clone.1, s32[]{:T(128)} %constant.122.clone.1, s32[]{:T(128)S(6)} %select_n.207) | dynamic-update-slice | bytes 1310724 | tf_op jit(solution)/shard_map/dynamic_update_slice | solution.py:56
  136.1 0.5 convolution_bitcast_fusion.5
  136.6 6.5 %dynamic_update_slice.29 = f32[1,1024,1280]{2,1,0:T(8,128)} dynamic-update-slice(f32[1,1024,1280]{2,1,0:T(8,128)} %dynamic_update_slice.28, f32[1,1024,160]{2,1,0:T(8,128)S(1)} %convolution_bitcast_fusion.5, s32[]{:T(128)} %constant.122.clone.1, s32[]{:T(128)} %constant.122.clone.1, s32[]{:T(128)S(6)} %select_n.209) | dynamic-update-slice | bytes 1310724 | tf_op jit(solution)/shard_map/dynamic_update_slice | solution.py:56
  143.1 0.5 convolution_bitcast_fusion.4
  143.6 6.3 %dynamic_update_slice.30 = f32[1,1024,1280]{2,1,0:T(8,128)} dynamic-update-slice(f32[1,1024,1280]{2,1,0:T(8,128)} %dynamic_update_slice.29, f32[1,1024,160]{2,1,0:T(8,128)S(1)} %convolution_bitcast_fusion.4, s32[]{:T(128)} %constant.122.clone.1, s32[]{:T(128)} %constant.122.clone.1, s32[]{:T(128)S(6)} %select_n.211) | dynamic-update-slice | bytes 1310724 | tf_op jit(solution)/shard_map/dynamic_update_slice | solution.py:56
  149.9 0.5 convolution_bitcast_fusion.3
  150.4 6.5 %dynamic_update_slice.31 = f32[1,1024,1280]{2,1,0:T(8,128)} dynamic-update-slice(f32[1,1024,1280]{2,1,0:T(8,128)} %dynamic_update_slice.30, f32[1,1024,160]{2,1,0:T(8,128)S(1)} %convolution_bitcast_fusion.3, s32[]{:T(128)} %constant.122.clone.1, s32[]{:T(128)} %constant.122.clone.1, s32[]{:T(128)S(6)} %select_n.213) | dynamic-update-slice | bytes 1310724 | tf_op jit(solution)/shard_map/dynamic_update_slice | solution.py:56
  156.9 0.5 convolution_bitcast_fusion.2
  157.4 6.5 %dynamic_update_slice.32 = f32[1,1024,1280]{2,1,0:T(8,128)} dynamic-update-slice(f32[1,1024,1280]{2,1,0:T(8,128)} %dynamic_update_slice.31, f32[1,1024,160]{2,1,0:T(8,128)S(1)} %convolution_bitcast_fusion.2, s32[]{:T(128)} %constant.122.clone.1, s32[]{:T(128)} %constant.122.clone.1, s32[]{:T(128)S(6)} %select_n.215) | dynamic-update-slice | bytes 1310724 | tf_op jit(solution)/shard_map/dynamic_update_slice | solution.py:56
  163.9 0.5 convolution_bitcast_fusion.1
  164.4 6.5 %dynamic_update_slice.33 = f32[1,1024,1280]{2,1,0:T(8,128)} dynamic-update-slice(f32[1,1024,1280]{2,1,0:T(8,128)} %dynamic_update_slice.32, f32[1,1024,160]{2,1,0:T(8,128)S(1)} %convolution_bitcast_fusion.1, s32[]{:T(128)} %constant.122.clone.1, s32[]{:T(128)} %constant.122.clone.1, s32[]{:T(128)S(6)} %select_n.217) | dynamic-update-slice | bytes 1310724 | tf_op jit(solution)/shard_map/dynamic_update_slice | solution.py:56
  170.8 0.5 convolution_bitcast_fusion
  171.3 6.0 %dynamic_update_slice.34 = f32[1,1024,1280]{2,1,0:T(8,128)} dynamic-update-slice(f32[1,1024,1280]{2,1,0:T(8,128)} %dynamic_update_slice.33, f32[1,1024,160]{2,1,0:T(8,128)S(1)} %convolution_bitcast_fusion, s32[]{:T(128)} %constant.122.clone.1, s32[]{:T(128)} %constant.122.clone.1, s32[]{:T(128)S(6)} %select_n.219) | dynamic-update-slice | bytes 1310724 | tf_op jit(solution)/shard_map/dynamic_update_slice | solution.py:56
  177.3 3.1 broadcast_multiply_fusion
  180.4 1.0 copy-done.1
  181.4 2.7 fusion.96
  184.1 1.3 fusion.35
  185.3 3.1 gather_fusion.1
  188.5 9.6 %gather_fusion = f32[1008,1280]{1,0:T(8,128)} fusion(f32[1024,1280]{1,0:T(8,128)} %fusion.35, s32[1024]{0:T(1024)S(1)} %pad_clamp_fusion.2), kind=kCustom, calls=%fused_computation | custom fusion | bytes 10325952 | tf_op jit(solution)/shard_map/jit(take_along_axis)/gather | solution.py:19
  198.0 5.1 %fusion.21 = bf16[1008,1,1280]{2,0,1:T(8,128)(2,1)S(1)} fusion(f32[1008,1280]{1,0:T(8,128)} %gather_fusion, pred[1008]{0:T(1024)(128)(4,1)S(1)} %compare_and_fusion, f32[16,1280]{1,0:T(8,128)S(1)} %gather_fusion.1, pred[16]{0:T(512)(128)(4,1)S(1)} %compare_and_fusion.1, s32[1008]{0:T(1024)S(1)} %bitcast.220, s32[16]{0:T(128)S(1)} %bitcast.230), kind=kOutput, calls=%fused_computation.32 | convolution fusion | flops 251633408 | bytes 7828480 | tf_op jit(solution)/shard_map/icr,ird->icd/dot_general | solution.py:22
  203.1 27.3 %fusion = bf16[256,1280]{1,0:T(8,128)(2,1)S(1)} fusion(bf16[1008,1,1280]{2,0,1:T(8,128)(2,1)S(1)} %fusion.21), kind=kCustom, calls=%all-reduce-scatter | all-reduce-scatter fusion | flops 1310721 | bytes 3236352
  230.4 4.4 %collective-permute-start.7 = (bf16[12,1280]{1,0:T(8,128)(2,1)S(1)}, bf16[12,1280]{1,0:T(8,128)(2,1)S(1)}, u32[]{:S(2)}, u32[]{:S(2)}) collective-permute-start(bf16[12,1280]{1,0:T(8,128)(2,1)S(1)} %slice.36), channel_id=1, source_target_pairs={{0,1},{1,2},{2,3},{4,5},{5,6},{6,7},{8,9},{9,10},{10,11},{12,13},{... | collective-permute-start | bytes 92168
  234.8 0.6 dynamic-slice.6
  236.1 1.1 concatenate.4
  237.2 0.4 fusion.44
  237.6 0.5 multiply_reduce_fusion
  238.1 0.4 multiply_convert_fusion
  238.5 2.1 copy.46
  240.7 39.4 %all-gather.10.cloned.1.call-done = bf16[1,1008,1280]{2,0,1:T(2,128)(2,1)} async-done(((bf16[1,252,1280]{2,0,1:T(2,128)(2,1)}), bf16[1,1008,1280]{2,0,1:T(2,128)(2,1)}) %all-gather.10.cloned.1.call-update) | async-done | bytes 2580496 | tf_op jit(solution)/shard_map/all_gather | solution.py:150
  280.1 12.9 %fusion.20 = bf16[1,1008,1280]{2,1,0:T(8,128)(2,1)} fusion(bf16[1280,1280]{0,1:T(8,128)(2,1)} %all-gather.14.cloned.1.call-done, bf16[1280,1280]{1,0:T(8,128)(2,1)} %all-gather.12.cloned.1.call-done, bf16[1,1008,1280]{2,0,1:T(2,128)(2,1)} %all-gather.10.cloned.1.call-done, f32[1280]{0:T(1024)S(1)} %copy-done.8), kind=kOutput, calls=%fused_computation.31 | convolution fusion | flops 6620221440 | bytes 11719680 | tf_op jit(solution)/shard_map/imf,fd->imd/dot_general | solution.py:159
  292.9 26.0 %fusion.1 = bf16[256,1280]{1,0:T(8,128)(2,1)S(1)} fusion(bf16[1,1008,1280]{2,1,0:T(8,128)(2,1)} %fusion.20), kind=kCustom, calls=%all-reduce-scatter.1 | all-reduce-scatter fusion | flops 1310721 | bytes 3236352
  319.0 4.4 %collective-permute-start.8 = (bf16[12,1280]{1,0:T(8,128)(2,1)S(1)}, bf16[12,1280]{1,0:T(8,128)(2,1)S(1)}, u32[]{:S(2)}, u32[]{:S(2)}) collective-permute-start(bf16[12,1280]{1,0:T(8,128)(2,1)S(1)} %slice.37), channel_id=1, source_target_pairs={{0,1},{1,2},{2,3},{4,5},{5,6},{6,7},{8,9},{9,10},{10,11},{12,13},{... | collective-permute-start | bytes 92168
  323.4 1.1 collective-permute-done.8
  324.5 1.0 concatenate.5
  325.5 1.3 add_convert_fusion.1
  (54 shorter events, 0.5 us)
Async XLA Ops:
  6.5 6.6 %copy-start.3 = (bf16[320,160]{0,1:T(8,128)(2,1)S(1)}, bf16[320,160]{0,1:T(8,128)(2,1)}, u32[]{:S(2)}) copy-start(bf16[320,160]{0,1:T(8,128)(2,1)} %param.16) | copy-start | bytes 307204
  6.5 12.0 %copy-start.9 = (s32[1,16]{1,0:T(1,128)S(1)}, s32[1,16]{1,0:T(1,128)}, u32[]{:S(2)}) copy-start(s32[1,16]{1,0:T(1,128)} %param.21) | copy-start | bytes 196
  6.5 12.0 %copy-start = (f32[1,1024]{1,0:T(1,128)S(1)}, f32[1,1024]{1,0:T(1,128)}, u32[]{:S(2)}) copy-start(f32[1,1024]{1,0:T(1,128)} %param.13) | copy-start | bytes 12292
  6.5 12.0 %copy-start.4 = (s32[1,1008]{1,0:T(1,128)S(1)}, s32[1,1008]{1,0:T(1,128)}, u32[]{:S(2)}) copy-start(s32[1,1008]{1,0:T(1,128)} %param.23) | copy-start | bytes 12100
  6.5 12.8 %copy-start.6 = (s32[1,16]{1,0:T(1,128)S(1)}, s32[1,16]{1,0:T(1,128)}, u32[]{:S(2)}) copy-start(s32[1,16]{1,0:T(1,128)} %param.22) | copy-start | bytes 196
  6.5 33.2 %all-gather.6.cloned.1.call-start = ((), (), s32[]{:S(2)}) async-start(), calls=%async_computation | async-start | bytes 3276800 | tf_op jit(solution)/shard_map/all_gather | solution.py:84
  11.6 86.2 %all-gather.8.cloned.1.call-start = ((), (), s32[]{:S(2)}) async-start(), calls=%async_computation.1 | async-start | bytes 3317760 | tf_op jit(solution)/shard_map/all_gather | solution.py:90
  12.3 228.4 %all-gather.12.cloned.1.call-start = ((), (), s32[]{:S(2)}) async-start(), calls=%async_computation.3 | async-start | bytes 3686400 | tf_op jit(solution)/shard_map/all_gather | solution.py:155
  13.1 227.7 %all-gather.14.cloned.1.call-start = ((), (), s32[]{:S(2)}) async-start(), calls=%async_computation.4 | async-start | bytes 3686400 | tf_op jit(solution)/shard_map/all_gather | solution.py:162
  13.1 8.2 %collective-permute-start = (bf16[320,160]{0,1:T(8,128)(2,1)S(1)}, bf16[320,160]{0,1:T(8,128)(2,1)S(1)}, u32[]{:S(2)}, u32[]{:S(2)}) collective-permute-start(bf16[320,160]{0,1:T(8,128)(2,1)S(1)} %copy-done.3), channel_id=1, source_target_pairs={{0,4},{4,8},{8,12},{12,16},{16,20},{20,24},{24,28},{28,0},{1,5},{5... | collective-permute-start | bytes 307208 | tf_op jit(solution)/shard_map/ppermute | solution.py:48
  15.2 6.1 %collective-permute-start.1 = (bf16[320,160]{0,1:T(8,128)(2,1)S(1)}, bf16[320,160]{0,1:T(8,128)(2,1)S(1)}, u32[]{:S(2)}, u32[]{:S(2)}) collective-permute-start(bf16[320,160]{0,1:T(8,128)(2,1)S(1)} %copy-done.3), channel_id=1, source_target_pairs={{4,0},{8,4},{12,8},{16,12},{20,16},{24,20},{28,24},{0,28},{5,1},{9... | collective-permute-start | bytes 307208 | tf_op jit(solution)/shard_map/ppermute | solution.py:49
  18.3 261.7 %all-gather.10.cloned.1.call-start = ((), (), s32[]{:S(2)}) async-start(), calls=%async_computation.2 | async-start | bytes 6451200 | tf_op jit(solution)/shard_map/all_gather | solution.py:150
  21.3 6.5 %collective-permute-start.2 = (bf16[320,160]{0,1:T(8,128)(2,1)S(1)}, bf16[320,160]{0,1:T(8,128)(2,1)S(1)}, u32[]{:S(2)}, u32[]{:S(2)}) collective-permute-start(bf16[320,160]{0,1:T(8,128)(2,1)S(1)} %collective-permute-done), channel_id=1, source_target_pairs={{0,4},{4,8},{8,12},{12,16},{16,20},{20,24},{24,28},{28,0},{1,5},{5... | collective-permute-start | bytes 307208 | tf_op jit(solution)/shard_map/ppermute | solution.py:65
  21.3 6.5 %collective-permute-start.3 = (bf16[320,160]{0,1:T(8,128)(2,1)S(1)}, bf16[320,160]{0,1:T(8,128)(2,1)S(1)}, u32[]{:S(2)}, u32[]{:S(2)}) collective-permute-start(bf16[320,160]{0,1:T(8,128)(2,1)S(1)} %collective-permute-done.1), channel_id=1, source_target_pairs={{4,0},{8,4},{12,8},{16,12},{20,16},{24,20},{28,24},{0,28},{5,1},{9... | collective-permute-start | bytes 307208 | tf_op jit(solution)/shard_map/ppermute | solution.py:66
  27.8 6.4 %collective-permute-start.4 = (bf16[320,160]{0,1:T(8,128)(2,1)S(1)}, bf16[320,160]{0,1:T(8,128)(2,1)S(1)}, u32[]{:S(2)}, u32[]{:S(2)}) collective-permute-start(bf16[320,160]{0,1:T(8,128)(2,1)S(1)} %collective-permute-done.2), channel_id=1, source_target_pairs={{0,4},{4,8},{8,12},{12,16},{16,20},{20,24},{24,28},{28,0},{1,5},{5... | collective-permute-start | bytes 307208 | tf_op jit(solution)/shard_map/ppermute | solution.py:65
  27.8 136.1 %collective-permute-start.5 = (bf16[320,160]{0,1:T(8,128)(2,1)S(1)}, bf16[320,160]{0,1:T(8,128)(2,1)S(1)}, u32[]{:S(2)}, u32[]{:S(2)}) collective-permute-start(bf16[320,160]{0,1:T(8,128)(2,1)S(1)} %collective-permute-done.3), channel_id=1, source_target_pairs={{4,0},{8,4},{12,8},{16,12},{20,16},{24,20},{28,24},{0,28},{5,1},{9... | collective-permute-start | bytes 307208 | tf_op jit(solution)/shard_map/ppermute | solution.py:66
  34.3 136.6 %collective-permute-start.6 = (bf16[320,160]{0,1:T(8,128)(2,1)S(1)}, bf16[320,160]{0,1:T(8,128)(2,1)S(1)}, u32[]{:S(2)}, u32[]{:S(2)}) collective-permute-start(bf16[320,160]{0,1:T(8,128)(2,1)S(1)} %collective-permute-done.4), channel_id=1, source_target_pairs={{0,4},{4,8},{8,12},{12,16},{16,20},{20,24},{24,28},{28,0},{1,5},{5... | collective-permute-start | bytes 307208 | tf_op jit(solution)/shard_map/ppermute | solution.py:65
  113.2 5.8 %copy-start.10 = (f32[4,512,1024]{2,1,0:T(8,128)S(1)}, f32[4,512,1024]{2,1,0:T(8,128)}, u32[]{:S(2)}) copy-start(f32[4,512,1024]{2,1,0:T(8,128)} %get-tuple-element.11) | copy-start | bytes 25165828
  177.3 4.1 %copy-start.1 = (f32[1,1024,1280]{2,1,0:T(8,128)S(1)}, f32[1,1024,1280]{2,1,0:T(8,128)}, u32[]{:S(2)}) copy-start(f32[1,1024,1280]{2,1,0:T(8,128)} %dynamic_update_slice.34) | copy-start | bytes 15728644
  181.4 2.7 copy-start.2
  203.1 31.7 %copy-start.7 = (u32[32]{0:T(128)S(1)}, u32[32]{0:T(128)}, u32[]{:S(2)}) copy-start(u32[32]{0:T(128)} %constant.160) | copy-start | bytes 388
  203.1 35.0 %copy-start.5 = (f32[1280]{0:T(1024)S(1)}, f32[1280]{0:T(1024)}, u32[]{:S(2)}) copy-start(f32[1280]{0:T(1024)} %param.17) | copy-start | bytes 15364
  230.4 5.7 %collective-permute-start.7 = (bf16[12,1280]{1,0:T(8,128)(2,1)S(1)}, bf16[12,1280]{1,0:T(8,128)(2,1)S(1)}, u32[]{:S(2)}, u32[]{:S(2)}) collective-permute-start(bf16[12,1280]{1,0:T(8,128)(2,1)S(1)} %slice.36), channel_id=1, source_target_pairs={{0,1},{1,2},{2,3},{4,5},{5,6},{6,7},{8,9},{9,10},{10,11},{12,13},{... | collective-permute-start | bytes 92168
  237.2 42.9 %copy-start.8 = (f32[1280]{0:T(1024)S(1)}, f32[1280]{0:T(1024)}, u32[]{:S(2)}) copy-start(f32[1280]{0:T(1024)} %param.19) | copy-start | bytes 15364
  319.0 5.5 %collective-permute-start.8 = (bf16[12,1280]{1,0:T(8,128)(2,1)S(1)}, bf16[12,1280]{1,0:T(8,128)(2,1)S(1)}, u32[]{:S(2)}, u32[]{:S(2)}) collective-permute-start(bf16[12,1280]{1,0:T(8,128)(2,1)S(1)} %slice.37), channel_id=1, source_target_pairs={{0,1},{1,2},{2,3},{4,5},{5,6},{6,7},{8,9},{9,10},{10,11},{12,13},{... | collective-permute-start | bytes 92168
Sparse Core Ops, SparseCore 0:
  11.7 27.9 all-gather.5
  41.9 55.8 all-gather.7
  100.0 60.0 all-gather.11
  162.1 60.0 all-gather.13
  240.8 39.2 all-gather.9
